TPU v7x, 32 devices: a whole 2x2x4 slice. The times are simulated.
32 devices in a mesh: dp: 8 (over z, y), expert: 2 (over core), tensor: 2 (over x).
Axes of the slice: x: 2, y: 2, z: 4, core: 2. Of those that a mesh axis runs over, the one named last changes fastest.
Arguments:
- dense_act: bfloat16 [2, 32, 512, 3584], P(None, 'dp', 'expert', 'tensor'), may hold values from -6 to 6
- dense_cot: bfloat16 [2, 32, 512, 3584], P(None, 'dp', ('expert', 'tensor')), may hold values from -6 to 6
- dense_proj_in: bfloat16 [2, 3584, 128], P(None, 'tensor'), may hold values from -0.09375 to 0.09375
- dense_proj_out: bfloat16 [2, 3584, 128], replicated, may hold values from -0.09375 to 0.09375
- expert_act: bfloat16 [32, 8, 64, 2560], P('dp', 'expert', None, 'tensor'), may hold values from -6 to 6
- expert_cot: bfloat16 [32, 8, 64, 3584], P('dp', 'expert', 'tensor'), may hold values from -6 to 6
- expert_proj_in: bfloat16 [2560, 128], P('tensor'), may hold values from -0.125 to 0.125
- expert_proj_out: bfloat16 [3584, 128], replicated, may hold values from -0.09375 to 0.09375
- dense_valid: float32 [2, 128, 128], replicated, may hold values from -0.0012207031 to 0.0012207031
- expert_valid: float32 [8, 128, 128], P('expert'), may hold values from -0.0012207031 to 0.0012207031
- domain_ids: int32 [32], P('dp'), may hold values from 0 to 63
- prior_mix: float32 [64], replicated, may hold values from 0.002 to 0.05
Outputs:
- log_mixture_weights: float32 [64], P('dp')
All inputs are finite; a program needn't handle non-finite values.
Results may differ from a plain program's by a relative error of at most 0.0003.
Values sent between devices are 32-bit elements; how exact they have to be, the bound alone decides.
A program may use at most 128 MiB of HBM per device.

v0:
```python
import jax
import jax.numpy as jnp
from jax import lax
from jax.sharding import PartitionSpec as P


def per_device(
    dense_act,
    dense_cot,
    dense_proj_in,
    dense_proj_out,
    expert_act,
    expert_cot,
    expert_proj_in,
    expert_proj_out,
    dense_valid,
    expert_valid,
    domain_ids,
    prior_mix,
):
    block = dense_act
    dense_update_vector = lax.psum_scatter(
        jnp.einsum("lmtd,ldr->tlmr", block, dense_proj_in, preferred_element_type=jnp.float32),
        "tensor",
        scatter_dimension=0,
        tiled=True,
    )
    dense_weight_matrix = jnp.einsum(
        "lmtd,ldr->tlmr", dense_cot, dense_proj_out, preferred_element_type=jnp.float32
    )
    dense_portion = jnp.einsum(
        "fquy,fquh->quyh", dense_update_vector, dense_weight_matrix, precision=lax.Precision.HIGHEST
    )
    block = expert_act
    expert_u = lax.psum_scatter(
        jnp.einsum("mecf,fr->cmer", block, expert_proj_in, preferred_element_type=jnp.float32),
        "tensor",
        scatter_dimension=0,
        tiled=True,
    )
    expert_weight_matrix = jnp.einsum(
        "mecd,dr->cmer", expert_cot, expert_proj_out, preferred_element_type=jnp.float32
    )
    expert_part = jnp.einsum(
        "cmer,cmes->mers", expert_u, expert_weight_matrix, precision=lax.Precision.HIGHEST
    )
    dense_full = lax.psum(dense_portion, ("expert", "tensor"))
    dense_score = jnp.sum(dense_full * dense_valid[:, None], axis=(0, 2, 3))
    expert_full = lax.psum(expert_part, "tensor")
    expert_local = jnp.sum(expert_full * expert_valid[None], axis=(1, 2, 3))
    score = dense_score + lax.psum(expert_local, "expert")
    domains = prior_mix.shape[0]
    onehot = (domain_ids[:, None] == jnp.arange(domains, dtype=jnp.int32)[None, :]).astype(
        jnp.float32
    )
    domain_part = jnp.dot(score, onehot, precision=lax.Precision.HIGHEST)
    share_tally_count = domains // lax.axis_size("dp")
    first_domain = lax.axis_index("dp") * share_tally_count
    previous_domain_share = lax.dynamic_slice_in_dim(prior_mix, first_domain, share_tally_count, 0)
    domain_total = lax.psum(domain_part, "dp")
    spread = jnp.sqrt(jnp.mean(domain_total * domain_total) + 1e-06)
    z_value = domain_total / spread
    mass = jnp.sum(prior_mix * jnp.exp(0.5 * z_value))
    z_share = lax.dynamic_slice_in_dim(z_value, first_domain, share_tally_count, 0)
    return jnp.log(previous_domain_share) + 0.5 * z_share - jnp.log(mass)


def solution(mesh):
    placed = (
        P(None, "dp", "expert", "tensor"),
        P(None, "dp", ("expert", "tensor"), None),
        P(None, "tensor", None),
        P(),
        P("dp", "expert", None, "tensor"),
        P("dp", "expert", "tensor", None),
        P("tensor", None),
        P(),
        P(),
        P("expert", None, None),
        P("dp"),
        P(),
    )
    return jax.shard_map(per_device, mesh=mesh, in_specs=placed, out_specs=P("dp"), check_vma=False)
```

profile of v0, /device:TPU:0, one launch (start us, length us, event | category | flops | bytes accessed | tf_op | source)
XLA Modules:
  0.0 206.4 jit_solution(693878961875852554)
XLA Ops:
  6.5 1.7 copy-done
  8.3 1.8 convolution_bitcast_fusion.1
  10.1 1.1 copy.18
  11.3 5.6 %convolution_bitcast_fusion = f32[256,2,4,128]{0,3,2,1:T(8,128)S(1)} fusion(bf16[2,4,256,1792]{3,2,1,0:T(8,128)(2,1)} %param.12, bf16[2,1792,128]{2,1,0:T(8,128)(2,1)S(1)} %copy-done.3), kind=kOutput, calls=%fused_computation.2 | convolution fusion | flops 939524096 | bytes 9306112 | tf_op jit(solution)/shard_map/lmtd,ldr->tlmr/dot_general | solution.py:23
  16.9 26.2 %copy.29 = f32[256,2,4,128]{2,3,1,0:T(8,128)} copy(f32[256,2,4,128]{0,3,2,1:T(8,128)S(1)} %convolution_bitcast_fusion) | data formatting | bytes 2097152
  43.2 29.4 %reshape.9 = f32[256,1024]{1,0:T(8,128)} reshape(f32[256,2,128,4]{3,2,1,0:T(8,128)} %bitcast.46) | data formatting | bytes 2097152
  72.6 0.6 dynamic-slice
  73.9 3.3 %fusion.6 = f32[128,4,4,32]{0,3,2,1:T(8,128)S(1)} fusion(bf16[4,4,32,3584]{3,2,1,0:T(8,128)(2,1)} %param.17, bf16[3584,128]{1,0:T(8,128)(2,1)S(1)} %copy-done.7), kind=kOutput, calls=%fused_computation.8 | convolution fusion | flops 469762048 | bytes 4849664 | tf_op jit(solution)/shard_map/mecd,dr->cmer/dot_general | solution.py:41
  77.2 1.0 constant_dynamic-slice_fusion
  78.2 2.8 %fusion.9 = f32[4,4,128,128]{3,2,1,0:T(8,128)} fusion(f32[128,4,4,32]{0,3,2,1:T(8,128)S(1)} %fusion.6, f32[32,4,4,128]{3,2,1,0:T(4,128)S(1)} %constant_dynamic-slice_fusion), kind=kOutput, calls=%fused_computation.12 | convolution fusion | flops 100663296 | bytes 1572864 | tf_op jit(solution)/shard_map/cmer,cmes->mers/dot_general | solution.py:44
  81.3 5.6 %fusion.2 = f32[128,2,4,128]{0,3,2,1:T(8,128)S(1)} fusion(bf16[2,4,128,3584]{3,2,1,0:T(8,128)(2,1)} %param.13, bf16[2,3584,128]{2,1,0:T(8,128)(2,1)S(1)} %copy-done.2), kind=kOutput, calls=%fused_computation.3 | convolution fusion | flops 939524096 | bytes 9699328 | tf_op jit(solution)/shard_map/lmtd,ldr->tlmr/dot_general | solution.py:28
  86.9 8.9 %reduce-scatter.4.cloned.1.call-done = f32[128,1024]{1,0:T(8,128)} async-done(((f32[256,1024]{1,0:T(8,128)}), f32[128,1024]{1,0:T(8,128)}) %reduce-scatter.4.cloned.1.call-update) | async-done | bytes 524304
  95.8 19.5 %reshape.10 = f32[128,2,128,4]{3,2,1,0:T(8,128)} reshape(f32[128,1024]{1,0:T(8,128)} %reduce-scatter.4.cloned.1.call-done) | data formatting | bytes 1048576
  115.3 13.2 %copy.16 = f32[128,2,4,128]{0,3,2,1:T(8,128)} copy(f32[128,2,4,128]{2,3,1,0:T(8,128)} %bitcast.47) | data formatting | bytes 1048576 | tf_op jit(solution)/shard_map/reduce_scatter | solution.py:22
  128.5 3.1 %fusion.12 = f32[2,4,128,128]{3,2,1,0:T(8,128)} fusion(f32[128,2,4,128]{0,3,2,1:T(8,128)} %copy.16, f32[128,2,4,128]{0,3,2,1:T(8,128)S(1)} %fusion.2), kind=kOutput, calls=%fused_computation.22 | convolution fusion | flops 201326592 | bytes 1572864 | tf_op jit(solution)/shard_map/fquy,fquh->quyh/dot_general | solution.py:31
  131.6 6.7 %all-reduce.7.cloned.1.call-done = f32[4,4,128,128]{3,2,1,0:T(8,128)} async-done(((f32[4,4,128,128]{3,2,1,0:T(8,128)}), f32[4,4,128,128]{3,2,1,0:T(8,128)}) %all-reduce.7.cloned.1.call-update) | async-done | bytes 1048592 | tf_op jit(solution)/shard_map/psum | solution.py:49
  138.3 1.4 multiply_reduce_fusion
  139.7 2.4 %psum.30 = f32[4]{0:T(128)S(1)} all-reduce(f32[4]{0:T(128)S(1)} %multiply_reduce_fusion), channel_id=1, replica_groups=mesh['dp'=8,'expert'=2,'tensor'=2] {'expert'}, use_global_device_ids=true, to_apply=%region_6.0 | all-reduce | flops 4 | bytes 32 | tf_op jit(solution)/shard_map/psum | solution.py:51
  142.1 31.8 %all-reduce.5.cloned.1.call-done = f32[2,4,128,128]{3,2,1,0:T(8,128)} async-done(((f32[2,4,128,128]{3,2,1,0:T(8,128)}), f32[2,4,128,128]{3,2,1,0:T(8,128)}) %all-reduce.5.cloned.1.call-update) | async-done | bytes 524304 | tf_op jit(solution)/shard_map/psum | solution.py:47
  173.9 1.2 multiply_reduce_fusion.1
  175.3 21.3 %psum.31 = f32[64]{0:T(128)S(1)} all-reduce(f32[64]{0:T(128)S(1)} %convolution_bitcast_fusion.2), channel_id=1, replica_groups=mesh['dp'=8,'expert'=2,'tensor'=2] {'dp'}, use_global_device_ids=true, to_apply=%region_7.0 | all-reduce | flops 64 | bytes 512 | tf_op jit(solution)/shard_map/psum | solution.py:60
  196.7 0.6 multiply_reduce_fusion.3
  198.0 0.6 multiply_reduce_fusion.2
  199.3 0.6 add_subtract_fusion
  (29 shorter events, 0.6 us)
Async XLA Ops:
  6.5 1.7 copy-start
  6.5 4.8 %copy-start.3 = (bf16[2,1792,128]{2,1,0:T(8,128)(2,1)S(1)}, bf16[2,1792,128]{2,1,0:T(8,128)(2,1)}, u32[]{:S(2)}) copy-start(bf16[2,1792,128]{2,1,0:T(8,128)(2,1)} %param.14) | copy-start | bytes 2752516
  6.5 70.6 %all-reduce.9.cloned.1.call-start = ((), (), s32[]{:S(2)}) async-start(), calls=%async_computation.4 | async-start | bytes 1048576
  11.3 84.6 %reduce-scatter.4.cloned.1.call-start = ((), (), s32[]{:S(2)}) async-start(), calls=%async_computation.3 | async-start | bytes 1572864
  43.2 29.4 %copy-start.9 = (u32[32]{0:T(128)S(1)}, u32[32]{0:T(128)}, u32[]{:S(2)}) copy-start(u32[32]{0:T(128)} %constant.29) | copy-start | bytes 388
  43.2 30.7 %copy-start.7 = (bf16[3584,128]{1,0:T(8,128)(2,1)S(1)}, bf16[3584,128]{1,0:T(8,128)(2,1)}, u32[]{:S(2)}) copy-start(bf16[3584,128]{1,0:T(8,128)(2,1)} %param.19) | copy-start | bytes 2752516
  72.6 65.7 %all-reduce.7.cloned.1.call-start = ((), (), s32[]{:S(2)}) async-start(), calls=%async_computation.2 | async-start | bytes 2097152 | tf_op jit(solution)/shard_map/psum | solution.py:49
  73.9 7.4 %copy-start.2 = (bf16[2,3584,128]{2,1,0:T(8,128)(2,1)S(1)}, bf16[2,3584,128]{2,1,0:T(8,128)(2,1)}, u32[]{:S(2)}) copy-start(bf16[2,3584,128]{2,1,0:T(8,128)(2,1)} %param.15) | copy-start | bytes 5505028
  81.0 92.9 %all-reduce.5.cloned.1.call-start = ((), (), s32[]{:S(2)}) async-start(), calls=%async_computation.1 | async-start | bytes 1048576 | tf_op jit(solution)/shard_map/psum | solution.py:47
  115.3 22.9 %copy-start.4 = (f32[4,128,128]{2,1,0:T(8,128)S(1)}, f32[4,128,128]{2,1,0:T(8,128)}, u32[]{:S(2)}) copy-start(f32[4,128,128]{2,1,0:T(8,128)} %param.21) | copy-start | bytes 786436
  115.3 58.6 %copy-start.5 = (f32[2,128,128]{2,1,0:T(8,128)S(1)}, f32[2,128,128]{2,1,0:T(8,128)}, u32[]{:S(2)}) copy-start(f32[2,128,128]{2,1,0:T(8,128)} %param.20) | copy-start | bytes 393220
  115.3 84.5 %copy-start.1 = (bf16[4,4,64,1280]{3,2,1,0:T(8,128)(2,1)S(1)}, bf16[4,4,64,1280]{3,2,1,0:T(8,128)(2,1)}, u32[]{:S(2)}) copy-start(bf16[4,4,64,1280]{3,2,1,0:T(8,128)(2,1)} %param.16) | copy-start | bytes 7864324
  128.5 46.6 %copy-start.8 = (s32[4]{0:T(128)S(1)}, s32[4]{0:T(128)}, u32[]{:S(2)}) copy-start(s32[4]{0:T(128)} %param.22) | copy-start | bytes 52
  128.5 69.5 %copy-start.6 = (f32[64]{0:T(128)S(1)}, f32[64]{0:T(128)}, u32[]{:S(2)}) copy-start(f32[64]{0:T(128)} %param.23) | copy-start | bytes 772
Sparse Core Ops, SparseCore 0:
  11.4 31.3 all-reduce.8
  72.7 23.1 reduce-scatter.3
  98.1 40.0 all-reduce.6
  140.5 33.4 all-reduce.4
where the time goes:
time: 207 us; the launch traced here: 206 us
  local copies, waits for them, and re-layouts  92.7 us (45%)
  waiting for transfers between devices  47.4 us (23%)
  blocking collectives  23.8 us (11%)
  matrix products  22.5 us (11%)
  between operations  15.3 us (7%)
  other arithmetic  4.44 us (2%)
    unnamed x25, local copies, waits for them, and re-layouts  78.4 us
    psum x1, waiting for transfers between devices, per_device(): dense_full = lax.psum(dense_portion, ('expert', 'tensor'))  31.8 us
    psum x1, blocking collectives, per_device(): domain_total = lax.psum(domain_part, 'dp')  21.3 us
    reduce_scatter x1, local copies, waits for them, and re-layouts, per_device(): lax.psum_scatter(jnp.einsum('lmtd,ldr->tlmr', block, dense_proj_in, prefe...  13.2 us
    unnamed x6, waiting for transfers between devices  8.98 us
    psum x1, waiting for transfers between devices, per_device(): expert_full = lax.psum(expert_part, 'tensor')  6.66 us
    dot_general x1, matrix products, per_device(): jnp.einsum('lmtd,ldr->tlmr', dense_cot, dense_proj_out, preferred_element...  5.64 us
    dot_general x1, matrix products, per_device(): jnp.einsum('lmtd,ldr->tlmr', block, dense_proj_in, preferred_element_type...  5.62 us
  transfers between devices with their start and end apart: 4, of which 3 were waited for; matrix products, arithmetic and copies ran while one was open for 54% of the time, Pallas kernels for 0%

commit v1 on v0

--- a/solution.py
+++ b/solution.py
@@ -44,7 +44,8 @@
     expert_part = jnp.einsum(
         "cmer,cmes->mers", expert_u, expert_weight_matrix, precision=lax.Precision.HIGHEST
     )
-    dense_full = lax.psum(dense_portion, ("expert", "tensor"))
+    one_axis = lax.psum(dense_portion, "tensor")
+    dense_full = lax.psum(one_axis, "expert")
     dense_score = jnp.sum(dense_full * dense_valid[:, None], axis=(0, 2, 3))
     expert_full = lax.psum(expert_part, "tensor")
     expert_local = jnp.sum(expert_full * expert_valid[None], axis=(1, 2, 3))

time: 207 us -> 237 us (1.14)
  waiting for transfers between devices: 47.4 us -> 77.8 us
    psum x2, waiting for transfers between devices: 38.4 us -> 68.6 us  [the longest x1 51.7 us: per_device(): one_axis = lax.psum(dense_portion, 'tensor')]
  transfers between devices with their start and end apart: 4 -> 4, of which waited for: 3 -> 3; matrix products, arithmetic and copies ran while one was open for 54% -> 32% of each run, Pallas kernels for 0% -> 0%
where the time goes in v1:
time: 237 us
  local copies, waits for them, and re-layouts  92.5 us (39%)
  waiting for transfers between devices  77.8 us (33%)
  blocking collectives  24.1 us (10%)
  matrix products  22.3 us (9%)
  between operations  15.3 us (6%)
  other arithmetic  4.44 us (2%)
    unnamed x25, local copies, waits for them, and re-layouts  78.4 us
    psum x1, waiting for transfers between devices, per_device(): one_axis = lax.psum(dense_portion, 'tensor')  51.7 us
    psum x1, blocking collectives, per_device(): domain_total = lax.psum(domain_part, 'dp')  21.6 us
    psum x1, waiting for transfers between devices, per_device(): dense_full = lax.psum(one_axis, 'expert')  16.9 us
    reduce_scatter x1, local copies, waits for them, and re-layouts, per_device(): lax.psum_scatter(jnp.einsum('lmtd,ldr->tlmr', block, dense_proj_in, prefe...  13 us
    unnamed x6, waiting for transfers between devices  9.25 us
    dot_general x1, matrix products, per_device(): jnp.einsum('lmtd,ldr->tlmr', dense_cot, dense_proj_out, preferred_element...  5.62 us
    dot_general x1, matrix products, per_device(): jnp.einsum('lmtd,ldr->tlmr', block, dense_proj_in, preferred_element_type...  5.62 us
  transfers between devices with their start and end apart: 4, of which 3 were waited for; matrix products, arithmetic and copies ran while one was open for 32% of the time, Pallas kernels for 0%

profile of v1, /device:TPU:0, one launch (start us, length us, event | category | flops | bytes accessed | tf_op | source)
XLA Modules:
  0.0 236.8 jit_solution(13737868965483552507)
XLA Ops:
  6.5 1.7 copy-done
  8.3 1.8 convolution_bitcast_fusion.1
  10.1 1.1 copy.18
  11.3 5.6 %convolution_bitcast_fusion = f32[256,2,4,128]{0,3,2,1:T(8,128)S(1)} fusion(bf16[2,4,256,1792]{3,2,1,0:T(8,128)(2,1)} %param.12, bf16[2,1792,128]{2,1,0:T(8,128)(2,1)S(1)} %copy-done.3), kind=kOutput, calls=%fused_computation.2 | convolution fusion | flops 939524096 | bytes 9306112 | tf_op jit(solution)/shard_map/lmtd,ldr->tlmr/dot_general | solution.py:23
  16.9 26.2 %copy.29 = f32[256,2,4,128]{2,3,1,0:T(8,128)} copy(f32[256,2,4,128]{0,3,2,1:T(8,128)S(1)} %convolution_bitcast_fusion) | data formatting | bytes 2097152
  43.2 29.4 %reshape.9 = f32[256,1024]{1,0:T(8,128)} reshape(f32[256,2,128,4]{3,2,1,0:T(8,128)} %bitcast.46) | data formatting | bytes 2097152
  72.8 0.6 dynamic-slice
  74.1 3.2 %fusion.6 = f32[128,4,4,32]{0,3,2,1:T(8,128)S(1)} fusion(bf16[4,4,32,3584]{3,2,1,0:T(8,128)(2,1)} %param.17, bf16[3584,128]{1,0:T(8,128)(2,1)S(1)} %copy-done.7), kind=kOutput, calls=%fused_computation.8 | convolution fusion | flops 469762048 | bytes 4849664 | tf_op jit(solution)/shard_map/mecd,dr->cmer/dot_general | solution.py:41
  77.2 5.6 %fusion.2 = f32[128,2,4,128]{0,3,2,1:T(8,128)S(1)} fusion(bf16[2,4,128,3584]{3,2,1,0:T(8,128)(2,1)} %param.13, bf16[2,3584,128]{2,1,0:T(8,128)(2,1)S(1)} %copy-done.2), kind=kOutput, calls=%fused_computation.3 | convolution fusion | flops 939524096 | bytes 9699328 | tf_op jit(solution)/shard_map/lmtd,ldr->tlmr/dot_general | solution.py:28
  82.9 1.0 constant_dynamic-slice_fusion
  83.9 2.8 %fusion.9 = f32[4,4,128,128]{3,2,1,0:T(8,128)} fusion(f32[128,4,4,32]{0,3,2,1:T(8,128)S(1)} %fusion.6, f32[32,4,4,128]{3,2,1,0:T(4,128)S(1)} %constant_dynamic-slice_fusion), kind=kOutput, calls=%fused_computation.12 | convolution fusion | flops 100663296 | bytes 1572864 | tf_op jit(solution)/shard_map/cmer,cmes->mers/dot_general | solution.py:44
  86.7 9.2 %reduce-scatter.4.cloned.1.call-done = f32[128,1024]{1,0:T(8,128)} async-done(((f32[256,1024]{1,0:T(8,128)}), f32[128,1024]{1,0:T(8,128)}) %reduce-scatter.4.cloned.1.call-update) | async-done | bytes 524304
  95.8 19.5 %reshape.10 = f32[128,2,128,4]{3,2,1,0:T(8,128)} reshape(f32[128,1024]{1,0:T(8,128)} %reduce-scatter.4.cloned.1.call-done) | data formatting | bytes 1048576
  115.3 13.0 %copy.16 = f32[128,2,4,128]{0,3,2,1:T(8,128)} copy(f32[128,2,4,128]{2,3,1,0:T(8,128)} %bitcast.47) | data formatting | bytes 1048576 | tf_op jit(solution)/shard_map/reduce_scatter | solution.py:22
  128.4 3.1 %fusion.12 = f32[2,4,128,128]{3,2,1,0:T(8,128)} fusion(f32[128,2,4,128]{0,3,2,1:T(8,128)} %copy.16, f32[128,2,4,128]{0,3,2,1:T(8,128)S(1)} %fusion.2), kind=kOutput, calls=%fused_computation.22 | convolution fusion | flops 201326592 | bytes 1572864 | tf_op jit(solution)/shard_map/fquy,fquh->quyh/dot_general | solution.py:31
  131.5 51.7 %all-reduce.10.cloned.1.call-done = (f32[2,4,128,128]{3,2,1,0:T(8,128)}, f32[4,4,128,128]{3,2,1,0:T(8,128)}) async-done(((f32[2,4,128,128]{3,2,1,0:T(8,128)}, f32[4,4,128,128]{3,2,1,0:T(8,128)}), (f32[2,4,128,128]{3,2,1,0:T(8,128)}, f32[4,4,128,128]{3,2,1,0:T(8,128)})) %all-reduce.10.cloned.1.call-update) | async-done | bytes 1572880 | tf_op jit(solution)/shard_map/psum | solution.py:47
  183.2 1.4 multiply_reduce_fusion
  184.7 2.4 %psum.38 = f32[4]{0:T(128)S(1)} all-reduce(f32[4]{0:T(128)S(1)} %multiply_reduce_fusion), channel_id=1, replica_groups=mesh['dp'=8,'expert'=2,'tensor'=2] {'expert'}, use_global_device_ids=true, to_apply=%region_7.0 | all-reduce | flops 4 | bytes 32 | tf_op jit(solution)/shard_map/psum | solution.py:52
  187.1 16.9 %all-reduce.6.cloned.1.call-done = f32[2,4,128,128]{3,2,1,0:T(8,128)} async-done(((f32[2,4,128,128]{3,2,1,0:T(8,128)}), f32[2,4,128,128]{3,2,1,0:T(8,128)}) %all-reduce.6.cloned.1.call-update) | async-done | bytes 524304 | tf_op jit(solution)/shard_map/psum | solution.py:48
  204.0 1.2 multiply_reduce_fusion.1
  205.4 21.6 %psum.39 = f32[64]{0:T(128)S(1)} all-reduce(f32[64]{0:T(128)S(1)} %convolution_bitcast_fusion.2), channel_id=1, replica_groups=mesh['dp'=8,'expert'=2,'tensor'=2] {'dp'}, use_global_device_ids=true, to_apply=%region_8.0 | all-reduce | flops 64 | bytes 512 | tf_op jit(solution)/shard_map/psum | solution.py:61
  227.1 0.6 multiply_reduce_fusion.3
  228.4 0.6 multiply_reduce_fusion.2
  229.7 0.6 add_subtract_fusion
  (29 shorter events, 0.6 us)
Async XLA Ops:
  6.5 1.7 copy-start
  6.5 4.8 %copy-start.3 = (bf16[2,1792,128]{2,1,0:T(8,128)(2,1)S(1)}, bf16[2,1792,128]{2,1,0:T(8,128)(2,1)}, u32[]{:S(2)}) copy-start(bf16[2,1792,128]{2,1,0:T(8,128)(2,1)} %param.14) | copy-start | bytes 2752516
  6.5 76.3 %all-reduce.8.cloned.1.call-start = ((), (), s32[]{:S(2)}) async-start(), calls=%async_computation.3 | async-start | bytes 1048576
  11.3 84.6 %reduce-scatter.4.cloned.1.call-start = ((), (), s32[]{:S(2)}) async-start(), calls=%async_computation.2 | async-start | bytes 1572864
  43.2 29.6 %copy-start.9 = (u32[32]{0:T(128)S(1)}, u32[32]{0:T(128)}, u32[]{:S(2)}) copy-start(u32[32]{0:T(128)} %constant.29) | copy-start | bytes 388
  43.2 30.9 %copy-start.7 = (bf16[3584,128]{1,0:T(8,128)(2,1)S(1)}, bf16[3584,128]{1,0:T(8,128)(2,1)}, u32[]{:S(2)}) copy-start(bf16[3584,128]{1,0:T(8,128)(2,1)} %param.19) | copy-start | bytes 2752516
  72.6 4.7 %copy-start.2 = (bf16[2,3584,128]{2,1,0:T(8,128)(2,1)S(1)}, bf16[2,3584,128]{2,1,0:T(8,128)(2,1)}, u32[]{:S(2)}) copy-start(bf16[2,3584,128]{2,1,0:T(8,128)(2,1)} %param.15) | copy-start | bytes 5505028
  72.6 110.6 %all-reduce.10.cloned.1.call-start = ((), (), s32[]{:S(2)}) async-start(), calls=%async_computation.4 | async-start | bytes 3145728 | tf_op jit(solution)/shard_map/psum | solution.py:47
  115.3 115.0 %copy-start.1 = (bf16[4,4,64,1280]{3,2,1,0:T(8,128)(2,1)S(1)}, bf16[4,4,64,1280]{3,2,1,0:T(8,128)(2,1)}, u32[]{:S(2)}) copy-start(bf16[4,4,64,1280]{3,2,1,0:T(8,128)(2,1)} %param.16) | copy-start | bytes 7864324
  128.3 54.9 %copy-start.4 = (f32[4,128,128]{2,1,0:T(8,128)S(1)}, f32[4,128,128]{2,1,0:T(8,128)}, u32[]{:S(2)}) copy-start(f32[4,128,128]{2,1,0:T(8,128)} %param.21) | copy-start | bytes 786436
  128.3 75.7 %copy-start.5 = (f32[2,128,128]{2,1,0:T(8,128)S(1)}, f32[2,128,128]{2,1,0:T(8,128)}, u32[]{:S(2)}) copy-start(f32[2,128,128]{2,1,0:T(8,128)} %param.20) | copy-start | bytes 393220
  128.3 76.9 %copy-start.8 = (s32[4]{0:T(128)S(1)}, s32[4]{0:T(128)}, u32[]{:S(2)}) copy-start(s32[4]{0:T(128)} %param.22) | copy-start | bytes 52
  128.3 100.0 %copy-start.6 = (f32[64]{0:T(128)S(1)}, f32[64]{0:T(128)}, u32[]{:S(2)}) copy-start(f32[64]{0:T(128)} %param.23) | copy-start | bytes 772
  131.5 72.6 %all-reduce.6.cloned.1.call-start = ((), (), s32[]{:S(2)}) async-start(), calls=%async_computation.1 | async-start | bytes 1048576 | tf_op jit(solution)/shard_map/psum | solution.py:48
Sparse Core Ops, SparseCore 0:
  11.4 31.3 all-reduce.7
  72.7 23.1 reduce-scatter.3
  131.6 51.5 all-reduce.9
  185.4 18.5 all-reduce.5
